TPU v7x, 128 devices: a whole 4x4x4 slice. The times are simulated.
128 devices in a mesh: rep: 4 (over z_hi, core), row: 4 (over x), col: 8 (over z_lo, y).
Axes of the slice: x: 4, y: 4, z: 4 (z_hi: 2, z_lo: 2; z = z_hi * 2 + z_lo), core: 2. Of those that a mesh axis runs over, the one named last changes fastest.
Arguments:
- grad_parts: bfloat16 [4, 16384, 6144], P('rep', ('row', 'col')), may hold values from -0.03125 to 0.03125, as said below
- statistic: float32 [6144, 6144], P('row', 'col'), may hold values from -150 to 150, as said below
Outputs:
- gram_matrix: float32 [6144, 6144], P('row', 'col')
- statistic_next: float32 [6144, 6144], P('row', 'col')
Inputs may be any that keep to these rules, and one draw needn't show every extreme that they name: Every entry of grad_parts has a magnitude between 2^-10 and 2^-5. statistic is symmetric and positive definite.
All inputs are finite; a program needn't handle non-finite values.
Results may differ from a plain program's by a relative error of at most 0.008.
Values may be sent and summed in bfloat16 or wider, within the bound.
A program may use at most 128 MiB of HBM per device.

v0:
```python
import jax
import jax.numpy as jnp
from jax import lax
from jax.sharding import PartitionSpec as P


def shards(grad_parts, statistic):
    own_part = grad_parts[0].astype(jnp.float32)
    summed = lax.psum_scatter(own_part.astype(jnp.bfloat16), "rep", scatter_dimension=0, tiled=True)
    rows_panel = lax.all_to_all(summed, "row", split_axis=1, concat_axis=0, tiled=True)
    cols_panel = lax.all_to_all(summed, "col", split_axis=1, concat_axis=0, tiled=True)
    row_count = lax.axis_size("row")
    col_count = lax.axis_size("col")
    quarter = summed.shape[0]
    right_whole = lax.all_gather(cols_panel, "row", axis=0, tiled=True)
    right_order = (
        right_whole.reshape(row_count, col_count, quarter, -1)
        .transpose(1, 0, 2, 3)
        .reshape(row_count * col_count * quarter, -1)
    )
    partial_tile = lax.dot_general(
        lax.all_gather(rows_panel, "col", axis=0, tiled=True),
        right_order,
        (((0,), (0,)), ((), ())),
        preferred_element_type=jnp.float32,
    )
    portion = lax.psum_scatter(partial_tile, "rep", scatter_dimension=0, tiled=True)
    gram_tile = lax.all_gather(portion, "rep", axis=0, tiled=True)
    return (gram_tile, 0.95 * statistic + 0.05 * gram_tile)


def solution(mesh):
    return jax.shard_map(
        shards,
        mesh=mesh,
        in_specs=(P("rep", ("row", "col"), None), P("row", "col")),
        out_specs=(P("row", "col"), P("row", "col")),
        check_vma=False,
    )
```

profile of v0, /device:TPU:1, one launch (start us, length us, event | category | flops | bytes accessed | tf_op | source)
XLA Modules:
  0.0 441.3 jit_solution(476243138658292207)
XLA Ops:
  7.2 0.0 reduce-scatter.7.cloned.1.call-start
  7.2 0.7 reduce-scatter.7.cloned.1.call-update
  7.9 0.0 all-gather.6.cloned.1.call-start
  7.9 71.7 %reduce-scatter.7.cloned.1.call-done = bf16[128,6144]{1,0:T(8,128)(2,1)} async-done(((bf16[512,6144]{1,0:T(8,128)(2,1)}), bf16[128,6144]{1,0:T(8,128)(2,1)}) %reduce-scatter.7.cloned.1.call-update) | async-done | bytes 1572880
  79.6 1.9 copy.14
  81.5 24.2 %all_to_all.38 = bf16[128,8,768]{0,2,1:T(8,128)(2,1)S(1)} all-to-all(bf16[128,8,768]{0,2,1:T(8,128)(2,1)S(1)} %bitcast.15), channel_id=1, replica_groups=mesh['rep'=4,'row'=4,'col'=8] {'col'}, dimensions={1} | all-to-all | bytes 3145728 | tf_op jit(solution)/shard_map/all_to_all | solution.py:11
  105.7 1.6 copy.11
  107.3 0.0 all-gather.6.cloned.1.call-update
  107.3 0.0 all-gather.4.cloned.1.call-start
  107.3 29.4 %all_to_all.39 = bf16[128,4,1536]{0,2,1:T(8,128)(2,1)S(1)} all-to-all(bf16[128,4,1536]{0,2,1:T(8,128)(2,1)S(1)} %bitcast.16), channel_id=1, replica_groups=mesh['rep'=4,'row'=4,'col'=8] {'row'}, dimensions={1} | all-to-all | bytes 3145728 | tf_op jit(solution)/shard_map/all_to_all | solution.py:10
  136.7 1.6 copy.10
  138.3 0.0 all-gather.4.cloned.1.call-update
  138.3 0.0 reduce-scatter.5.cloned.1.call-start
  138.4 44.5 %all-gather.6.cloned.1.call-done = bf16[4096,768]{1,0:T(8,128)(2,1)} async-done(((bf16[1024,768]{1,0:T(8,128)(2,1)}), bf16[4096,768]{1,0:T(8,128)(2,1)}) %all-gather.6.cloned.1.call-update) | async-done | bytes 6291472 | tf_op jit(solution)/shard_map/all_gather | solution.py:15
  182.9 6.0 %copy.12 = bf16[4,8,128,768]{3,2,0,1:T(8,128)(2,1)} copy(bf16[4,8,128,768]{3,2,1,0:T(8,128)(2,1)} %bitcast.18) | data formatting | bytes 12582912 | tf_op jit(solution)/shard_map/reshape | solution.py:17
  188.9 123.7 %all-gather.4.cloned.1.call-done = bf16[4096,1536]{1,0:T(8,128)(2,1)} async-done(((bf16[512,1536]{1,0:T(8,128)(2,1)}), bf16[4096,1536]{1,0:T(8,128)(2,1)}) %all-gather.4.cloned.1.call-update) | async-done | bytes 12582928 | tf_op jit(solution)/shard_map/all_gather | solution.py:22
  312.6 16.4 %fusion = f32[1536,768]{1,0:T(8,128)} fusion(bf16[4096,1536]{1,0:T(8,128)(2,1)} %all-gather.4.cloned.1.call-done, bf16[4096,768]{1,0:T(8,128)(2,1)} %bitcast.19), kind=kOutput, calls=%fused_computation.1 | convolution fusion | flops 9663676416 | bytes 23592960 | tf_op jit(solution)/shard_map/dot_general | solution.py:21
  328.9 0.0 reduce-scatter.5.cloned.1.call-update
  328.9 0.0 all-gather.8.cloned.1.call-start
  329.0 53.8 %reduce-scatter.5.cloned.1.call-done = f32[384,768]{1,0:T(8,128)} async-done(((f32[1536,768]{1,0:T(8,128)}), f32[384,768]{1,0:T(8,128)}) %reduce-scatter.5.cloned.1.call-update) | async-done | bytes 1179664 | tf_op jit(solution)/shard_map/reduce_scatter | solution.py:27
  382.8 0.0 all-gather.8.cloned.1.call-update
  382.8 42.9 %all-gather.8.cloned.1.call-done = f32[1536,768]{1,0:T(8,128)} async-done(((f32[384,768]{1,0:T(8,128)}), f32[1536,768]{1,0:T(8,128)}) %all-gather.8.cloned.1.call-update) | async-done | bytes 4718608 | tf_op jit(solution)/shard_map/all_gather | solution.py:28
  425.7 0.0 copy-start
  425.7 6.8 %multiply_add_fusion = f32[1536,768]{1,0:T(8,128)} fusion(f32[1536,768]{1,0:T(8,128)} %all-gather.8.cloned.1.call-done, f32[1536,768]{1,0:T(8,128)} %param.3), kind=kLoop, calls=%fused_computation | loop fusion | flops 3538944 | bytes 14155776 | tf_op jit(solution)/shard_map/add | solution.py:29
  432.6 0.0 copy-done
  432.6 2.2 copy.17
Async XLA Ops:
  7.2 72.4 %reduce-scatter.7.cloned.1.call-start = ((), (), s32[]{:S(2)}) async-start(), calls=%async_computation.8 | async-start | bytes 7864320
  7.9 175.0 %all-gather.6.cloned.1.call-start = ((), (), s32[]{:S(2)}) async-start(), calls=%async_computation.5 | async-start | bytes 7864320 | tf_op jit(solution)/shard_map/all_gather | solution.py:15
  107.3 205.3 %all-gather.4.cloned.1.call-start = ((), (), s32[]{:S(2)}) async-start(), calls=%async_computation.4 | async-start | bytes 14155776 | tf_op jit(solution)/shard_map/all_gather | solution.py:22
  138.3 244.5 %reduce-scatter.5.cloned.1.call-start = ((), (), s32[]{:S(2)}) async-start(), calls=%async_computation.6 | async-start | bytes 5898240 | tf_op jit(solution)/shard_map/reduce_scatter | solution.py:27
  328.9 96.8 %all-gather.8.cloned.1.call-start = ((), (), s32[]{:S(2)}) async-start(), calls=%async_computation.7 | async-start | bytes 5898240 | tf_op jit(solution)/shard_map/all_gather | solution.py:28
  425.7 6.9 %copy-start = (f32[1536,768]{1,0:T(8,128)S(1)}, f32[1536,768]{1,0:T(8,128)}, u32[]{:S(2)}) copy-start(f32[1536,768]{1,0:T(8,128)} %all-gather.8.cloned.1.call-done) | copy-start | bytes 14155780
Sparse Core Ops, SparseCore 0:
  10.6 68.9 reduce-scatter.6
  107.4 75.4 all-gather.5
  185.1 127.4 all-gather.3
  329.1 53.6 reduce-scatter.4
  384.3 41.3 all-gather.7
where the time goes:
time: 442 us; the launch traced here: 441 us
  waiting for transfers between devices  337 us (76%)
  blocking collectives  53.6 us (12%)
  matrix products  16.4 us (4%)
  between operations  13.8 us (3%)
  local copies, waits for them, and re-layouts  13.3 us (3%)
  other arithmetic  6.85 us (2%)
    all_gather x1, waiting for transfers between devices, shards(): lax.all_gather(rows_panel, 'col', axis=0, tiled=True)  124 us
    unnamed x6, waiting for transfers between devices  72.4 us
    reduce_scatter x1, waiting for transfers between devices, shards(): lax.psum_scatter(partial_tile, 'rep', scatter_dimension=0, tiled=True)  53.8 us
    all_gather x1, waiting for transfers between devices, shards(): right_whole = lax.all_gather(cols_panel, 'row', axis=0, tiled=True)  44.5 us
    all_gather x1, waiting for transfers between devices, shards(): gram_tile = lax.all_gather(portion, 'rep', axis=0, tiled=True)  42.9 us
    all_to_all x1, blocking collectives, shards(): lax.all_to_all(summed, 'row', split_axis=1, concat_axis=0, tiled=True)  29.4 us
    all_to_all x1, blocking collectives, shards(): lax.all_to_all(summed, 'col', split_axis=1, concat_axis=0, tiled=True)  24.2 us
    dot_general x1, matrix products, shards(): lax.dot_general(lax.all_gather(rows_panel, 'col', axis=0, tiled=True), ri...  16.4 us
  transfers between devices with their start and end apart: 5, of which 5 were waited for; matrix products, arithmetic and copies ran while one was open for 2% of the time, Pallas kernels for 0%

commit v1 on v0

--- a/solution.py
+++ b/solution.py
@@ -2,6 +2,18 @@
 import jax.numpy as jnp
 from jax import lax
 from jax.sharding import PartitionSpec as P
+
+
+def take_the_frame(arr, which_axis):
+    count_all = lax.axis_size(which_axis)
+    tray = tuple(((nth, (nth + 1) % count_all) for nth in range(count_all)))
+    met_up = [None] * count_all
+    met_up[count_all - 1] = arr
+    for i in range(count_all - 2, -1, -1):
+        met_up[i] = lax.ppermute(met_up[i + 1], which_axis, tray)
+    far_arr = jnp.concatenate(met_up, axis=0)
+    block_out = (lax.axis_index(which_axis) + 1) * arr.shape[0]
+    return jnp.roll(far_arr, block_out, axis=0)
 
 
 def shards(grad_parts, statistic):
@@ -12,7 +24,7 @@
     row_count = lax.axis_size("row")
     col_count = lax.axis_size("col")
     quarter = summed.shape[0]
-    right_whole = lax.all_gather(cols_panel, "row", axis=0, tiled=True)
+    right_whole = take_the_frame(cols_panel, "row")
     right_order = (
         right_whole.reshape(row_count, col_count, quarter, -1)
         .transpose(1, 0, 2, 3)

time: 442 us -> 404 us (0.914)
  waiting for transfers between devices: 337 us -> 266 us
  local copies, waits for them, and re-layouts: 13.3 us -> 44.3 us
    all_gather x1, waiting for transfers between devices: 124 us -> 0.01 us  [shards(): lax.all_gather(rows_panel, 'col', axis=0, tiled=True)]
    ppermute x0 -> x3, waiting for transfers between devices: none -> 93.6 us  [take_the_frame(): met_up[i] = lax.ppermute(met_up[i + 1], which_axis, tray)]
    all_gather x1 -> x0, waiting for transfers between devices: 44.5 us -> none  [shards(): right_whole = lax.all_gather(cols_panel, 'row', axis=0, tiled=True)]
    unnamed x4 -> x11, local copies, waits for them, and re-layouts: 4.1 us -> 34.5 us
    reduce_scatter x1, waiting for transfers between devices: 53.8 us -> 63.7 us  [shards(): lax.psum_scatter(partial_tile, 'rep', scatter_dimension=0, tiled=True)]
    all_to_all x1, blocking collectives: 24.2 us -> 31.5 us  [shards(): lax.all_to_all(summed, 'col', split_axis=1, concat_axis=0, tiled=True)]
    all_gather x1, waiting for transfers between devices: 42.9 us -> 36.9 us  [shards(): gram_tile = lax.all_gather(portion, 'rep', axis=0, tiled=True)]
    reshape x1 -> x0, local copies, waits for them, and re-layouts: 6.04 us -> none  [shards(): right_whole.reshape(row_count, col_count, quarter, -1).transpose(1, 0, 2, 3)]
  transfers between devices with their start and end apart: 5 -> 7, of which waited for: 5 -> 6; matrix products, arithmetic and copies ran while one was open for 2% -> 7% of each run, Pallas kernels for 0% -> 0%
where the time goes in v1:
time: 404 us; the launch traced here: 403 us
  waiting for transfers between devices  266 us (66%)
  blocking collectives  55 us (14%)
  local copies, waits for them, and re-layouts  44.3 us (11%)
  matrix products  16.3 us (4%)
  between operations  13.8 us (3%)
  other arithmetic  7.07 us (2%)
    ppermute x3, waiting for transfers between devices, take_the_frame(): met_up[i] = lax.ppermute(met_up[i + 1], which_axis, tray)  93.6 us
    unnamed x5, waiting for transfers between devices  72.4 us
    reduce_scatter x1, waiting for transfers between devices, shards(): lax.psum_scatter(partial_tile, 'rep', scatter_dimension=0, tiled=True)  63.7 us
    all_gather x1, waiting for transfers between devices, shards(): gram_tile = lax.all_gather(portion, 'rep', axis=0, tiled=True)  36.9 us
    unnamed x11, local copies, waits for them, and re-layouts  34.5 us
    all_to_all x1, blocking collectives, shards(): lax.all_to_all(summed, 'col', split_axis=1, concat_axis=0, tiled=True)  31.5 us
    all_to_all x1, blocking collectives, shards(): lax.all_to_all(summed, 'row', split_axis=1, concat_axis=0, tiled=True)  23.5 us
    dot_general x1, matrix products, shards(): lax.dot_general(lax.all_gather(rows_panel, 'col', axis=0, tiled=True), ri...  16.3 us
  transfers between devices with their start and end apart: 7, of which 6 were waited for; matrix products, arithmetic and copies ran while one was open for 7% of the time, Pallas kernels for 0%

profile of v1, /device:TPU:1, one launch (start us, length us, event | category | flops | bytes accessed | tf_op | source)
XLA Modules:
  0.0 403.1 jit_solution(6673578233469608987)
XLA Ops:
  7.2 0.0 reduce-scatter.7.cloned.1.call-start
  7.2 0.7 reduce-scatter.7.cloned.1.call-update
  7.9 0.0 all-gather.3.cloned.1.call-start
  7.9 71.7 %reduce-scatter.7.cloned.1.call-done = bf16[128,6144]{1,0:T(8,128)(2,1)} async-done(((bf16[512,6144]{1,0:T(8,128)(2,1)}), bf16[128,6144]{1,0:T(8,128)(2,1)}) %reduce-scatter.7.cloned.1.call-update) | async-done | bytes 1572880
  79.6 1.9 copy.25
  81.5 23.5 %all_to_all.38 = bf16[128,4,1536]{0,2,1:T(8,128)(2,1)S(1)} all-to-all(bf16[128,4,1536]{0,2,1:T(8,128)(2,1)S(1)} %bitcast.21), channel_id=1, replica_groups=mesh['rep'=4,'row'=4,'col'=8] {'row'}, dimensions={1} | all-to-all | bytes 3145728 | tf_op jit(solution)/shard_map/all_to_all | solution.py:22
  105.0 1.6 copy.20
  106.5 0.0 all-gather.3.cloned.1.call-update
  106.5 0.0 reduce-scatter.5.cloned.1.call-start
  106.6 31.5 %all_to_all.39 = bf16[128,8,768]{0,2,1:T(8,128)(2,1)S(1)} all-to-all(bf16[128,8,768]{0,2,1:T(8,128)(2,1)S(1)} %bitcast.22), channel_id=1, replica_groups=mesh['rep'=4,'row'=4,'col'=8] {'col'}, dimensions={1} | all-to-all | bytes 3145728 | tf_op jit(solution)/shard_map/all_to_all | solution.py:23
  138.1 0.7 copy.18
  138.8 0.1 collective-permute-start
  138.9 27.7 %collective-permute-done = bf16[1024,768]{1,0:T(8,128)(2,1)S(1)} collective-permute-done((bf16[1024,768]{1,0:T(8,128)(2,1)S(1)}, bf16[1024,768]{1,0:T(8,128)(2,1)S(1)}, u32[]{:S(2)}, u32[]{:S(2)}) %collective-permute-start) | collective-permute-done | bytes 1572896 | tf_op jit(solution)/shard_map/ppermute | solution.py:13
  166.6 0.0 collective-permute-start.1
  166.6 33.0 %collective-permute-done.1 = bf16[1024,768]{1,0:T(8,128)(2,1)} collective-permute-done((bf16[1024,768]{1,0:T(8,128)(2,1)S(1)}, bf16[1024,768]{1,0:T(8,128)(2,1)}, u32[]{:S(2)}, u32[]{:S(2)}) %collective-permute-start.1) | collective-permute-done | bytes 1572896 | tf_op jit(solution)/shard_map/ppermute | solution.py:13
  199.6 0.0 collective-permute-start.2
  199.6 32.9 %collective-permute-done.2 = bf16[1024,768]{1,0:T(8,128)(2,1)} collective-permute-done((bf16[1024,768]{1,0:T(8,128)(2,1)}, bf16[1024,768]{1,0:T(8,128)(2,1)}, u32[]{:S(2)}, u32[]{:S(2)}) %collective-permute-start.2) | collective-permute-done | bytes 1572896 | tf_op jit(solution)/shard_map/ppermute | solution.py:13
  232.5 2.7 constant_dynamic-update-slice_fusion.7
  235.1 2.7 constant_dynamic-update-slice_fusion.6
  237.8 1.2 constant_dynamic-update-slice_fusion.5
  239.1 1.3 constant_dynamic-update-slice_fusion.4
  240.3 2.7 constant_dynamic-update-slice_fusion.3
  243.0 2.6 constant_dynamic-update-slice_fusion.2
  245.7 1.3 constant_dynamic-update-slice_fusion.1
  247.0 1.3 constant_dynamic-update-slice_fusion
  248.2 3.2 constant_dynamic-slice_fusion
  251.4 3.0 copy.19
  254.4 0.0 all-gather.3.cloned.1.call-done
  254.4 16.3 %convolution_bitcast_fusion = f32[1536,768]{0,1:T(8,128)} fusion(bf16[4096,768]{1,0:T(8,128)(2,1)} %bitcast.24, bf16[4096,1536]{1,0:T(8,128)(2,1)} %all-gather.3.cloned.1.call-done), kind=kOutput, calls=%fused_computation.1 | convolution fusion | flops 9663676416 | bytes 23592960 | tf_op jit(solution)/shard_map/dot_general | solution.py:33
  270.7 0.0 reduce-scatter.5.cloned.1.call-update
  270.8 0.0 all-gather.5.cloned.1.call-start
  270.8 63.7 %reduce-scatter.5.cloned.1.call-done = f32[384,768]{0,1:T(8,128)} async-done(((f32[1536,768]{0,1:T(8,128)}), f32[384,768]{0,1:T(8,128)}) %reduce-scatter.5.cloned.1.call-update) | async-done | bytes 1179664 | tf_op jit(solution)/shard_map/reduce_scatter | solution.py:39
  334.5 0.0 all-gather.5.cloned.1.call-update
  334.5 6.0 %copy.21 = f32[1536,768]{0,1:T(8,128)} copy(f32[1536,768]{1,0:T(8,128)} %param.3) | data formatting | bytes 9437184 | tf_op args[1]
  340.6 36.9 %all-gather.5.cloned.1.call-done = f32[1536,768]{0,1:T(8,128)} async-done(((f32[384,768]{0,1:T(8,128)}), f32[1536,768]{0,1:T(8,128)}) %all-gather.5.cloned.1.call-update) | async-done | bytes 4718608 | tf_op jit(solution)/shard_map/all_gather | solution.py:40
  377.4 7.1 %multiply_add_fusion = f32[1536,768]{0,1:T(8,128)} fusion(f32[1536,768]{0,1:T(8,128)} %all-gather.5.cloned.1.call-done, f32[1536,768]{0,1:T(8,128)} %copy.21), kind=kLoop, calls=%fused_computation | loop fusion | flops 3538944 | bytes 14155776 | tf_op jit(solution)/shard_map/add | solution.py:41
  384.5 6.0 %copy.23 = f32[1536,768]{1,0:T(8,128)} copy(f32[1536,768]{0,1:T(8,128)} %multiply_add_fusion) | data formatting | bytes 9437184
  390.5 6.0 %copy.22 = f32[1536,768]{1,0:T(8,128)} copy(f32[1536,768]{0,1:T(8,128)} %all-gather.5.cloned.1.call-done) | data formatting | bytes 9437184
Async XLA Ops:
  7.2 72.4 %reduce-scatter.7.cloned.1.call-start = ((), (), s32[]{:S(2)}) async-start(), calls=%async_computation.7 | async-start | bytes 7864320
  7.9 246.5 %all-gather.3.cloned.1.call-start = ((), (), s32[]{:S(2)}) async-start(), calls=%async_computation.4 | async-start | bytes 14155776 | tf_op jit(solution)/shard_map/all_gather | solution.py:34
  106.5 227.9 %reduce-scatter.5.cloned.1.call-start = ((), (), s32[]{:S(2)}) async-start(), calls=%async_computation.5 | async-start | bytes 5898240 | tf_op jit(solution)/shard_map/reduce_scatter | solution.py:39
  138.8 27.8 %collective-permute-start = (bf16[1024,768]{1,0:T(8,128)(2,1)S(1)}, bf16[1024,768]{1,0:T(8,128)(2,1)S(1)}, u32[]{:S(2)}, u32[]{:S(2)}) collective-permute-start(bf16[1024,768]{1,0:T(8,128)(2,1)S(1)} %bitcast.18), channel_id=1, source_target_pairs={{0,8},{8,16},{16,24},{24,0},{1,9},{9,17},{17,25},{25,1},{2,10},{10... | collective-permute-start | bytes 4718600 | tf_op jit(solution)/shard_map/ppermute | solution.py:13
  166.6 33.0 %collective-permute-start.1 = (bf16[1024,768]{1,0:T(8,128)(2,1)S(1)}, bf16[1024,768]{1,0:T(8,128)(2,1)}, u32[]{:S(2)}, u32[]{:S(2)}) collective-permute-start(bf16[1024,768]{1,0:T(8,128)(2,1)S(1)} %collective-permute-done), channel_id=1, source_target_pairs={{0,8},{8,16},{16,24},{24,0},{1,9},{9,17},{17,25},{25,1},{2,10},{10... | collective-permute-start | bytes 4718600 | tf_op jit(solution)/shard_map/ppermute | solution.py:13
  199.6 32.9 %collective-permute-start.2 = (bf16[1024,768]{1,0:T(8,128)(2,1)}, bf16[1024,768]{1,0:T(8,128)(2,1)}, u32[]{:S(2)}, u32[]{:S(2)}) collective-permute-start(bf16[1024,768]{1,0:T(8,128)(2,1)} %collective-permute-done.1), channel_id=1, source_target_pairs={{0,8},{8,16},{16,24},{24,0},{1,9},{9,17},{17,25},{25,1},{2,10},{10... | collective-permute-start | bytes 4718600 | tf_op jit(solution)/shard_map/ppermute | solution.py:13
  270.8 106.7 %all-gather.5.cloned.1.call-start = ((), (), s32[]{:S(2)}) async-start(), calls=%async_computation.6 | async-start | bytes 5898240 | tf_op jit(solution)/shard_map/all_gather | solution.py:40
Sparse Core Ops, SparseCore 0:
  10.6 68.9 reduce-scatter.6
  106.7 144.1 all-gather.2
  270.9 63.5 reduce-scatter.4
  336.0 41.3 all-gather.4
